TPU v7x, 128 devices: a whole 4x4x4 slice. The times are simulated.
128 devices in a mesh: bond: 32 (over x, z_lo, y), outer: 4 (over z_hi, core).
Axes of the slice: x: 4, y: 4, z: 4 (z_hi: 2, z_lo: 2; z = z_hi * 2 + z_lo), core: 2. Of those that a mesh axis runs over, the one named last changes fastest.
Arguments:
- upper: bfloat16 [128, 128, 128], P(None, 'bond'), may hold values from -4 to 4
- lower: bfloat16 [128, 128, 8, 128], P(None, 'bond', 'outer'), may hold values from -4 to 4
- isometry: bfloat16 [16384, 128], P(('bond', 'outer')), may hold values from -0.046875 to 0.046875
Outputs:
- coarse: float32 [128, 8, 128], P('bond', 'outer')
All inputs are finite; a program needn't handle non-finite values.
Results may differ from a plain program's by a relative error of at most 0.004.
Values may be sent and summed in bfloat16 or wider, within the bound.
No kernel may reach another device: no remote copies, remote signals or barrier semaphores. Data moves between devices by JAX's collectives and lax.ppermute only.
A program may use at most 64 MiB of HBM per device.

v0:
```python
import jax
import jax.numpy as jnp
from jax import lax
from jax.sharding import PartitionSpec as P


def from_everyone(value, axis):
    peers = lax.axis_size(axis)
    return lax.all_to_all(
        jnp.broadcast_to(value[None], (peers, *value.shape)), axis, 0, 0, tiled=True
    )


def laid_out(tiles, dim):
    dims = list(tiles.shape[1:])
    dims[dim] *= tiles.shape[0]
    return jnp.moveaxis(tiles, 0, dim).reshape(dims)


def gathered_copies(value, axis, dim):
    tiles = from_everyone(value, axis)
    return laid_out(tiles, dim)


def side_by_side(arrays, axis, split_dim, concat_dim, along):
    columns = [a.reshape(*a.shape[:along], -1) for a in arrays]
    both = jnp.concatenate(columns, axis=along)
    whole, at, gathered = (
        lax.all_to_all(both, axis, split_axis=split_dim, concat_axis=concat_dim, tiled=True),
        0,
        [],
    )
    for a, column in zip(arrays, columns):
        slab = whole[..., at : at + column.shape[along]]
        gathered.append(slab.reshape(*slab.shape[:along], *a.shape[along:]))
        at += column.shape[along]
    return tuple(gathered)


def split_up(value, dim, peers):
    before, after = (value.shape[:dim], value.shape[dim + 1 :])
    return jnp.moveaxis(value.reshape(*before, peers, -1, *after), dim, 0)


def sum_at_owner(value, axis, dim):
    peers = lax.axis_size(axis)
    tiles = lax.all_to_all(split_up(value, dim, peers), axis, 0, 0, tiled=True)
    return jnp.sum(tiles, axis=0)


def on_device(upper, lower, isometry):
    grouped = gathered_copies(isometry, "outer", 0)
    gathered = lax.all_gather(grouped, "bond", axis=0, tiled=True)
    upper_local, lower_local = side_by_side((upper, lower), "bond", 0, 1, 2)
    width = gathered.shape[1]
    iso_full = gathered.reshape(width, width, width)
    members = upper_local.shape[0]
    lower_count = lower_local.shape[2]
    own_rows = width // lax.axis_size("bond")

    def member(index, total):
        upper_slab = lax.dynamic_index_in_dim(upper_local, index, 0, keepdims=False)
        lower_slab = lax.dynamic_index_in_dim(lower_local, index, 0, keepdims=False)
        joined = jnp.einsum(
            "lr,lkx->rkx", upper_slab, iso_full, preferred_element_type=jnp.float32
        ).astype(jnp.bfloat16)
        paired = jnp.einsum(
            "rkx,kds->drxs", joined, lower_slab, preferred_element_type=jnp.float32
        ).astype(jnp.bfloat16)
        return total + jnp.einsum(
            "drxs,rsy->xdy", paired, iso_full, preferred_element_type=jnp.float32
        )

    start_total = jnp.zeros((own_rows * lax.axis_size("bond"), lower_count, width), jnp.float32)
    return sum_at_owner(lax.fori_loop(0, members, member, start_total), "bond", 0)


def solution(mesh):
    return jax.shard_map(
        on_device,
        mesh=mesh,
        in_specs=(
            P(None, "bond", None),
            P(None, "bond", "outer", None),
            P(("bond", "outer"), None),
        ),
        out_specs=P("bond", "outer", None),
        check_vma=False,
    )
```

profile of v0, /device:TPU:0, one launch (start us, length us, event | category | flops | bytes accessed | tf_op | source)
XLA Modules:
  0.0 266.1 jit_solution(133806632198661356)
XLA Ops:
  6.5 0.0 all-gather.2.cloned.1.call-start
  6.5 0.8 broadcast_in_dim.10
  7.3 11.3 %all_to_all.28 = bf16[4,128,128]{2,1,0:T(8,128)(2,1)} all-to-all(bf16[4,128,128]{2,1,0:T(8,128)(2,1)S(1)} %broadcast_in_dim.10), channel_id=1, replica_groups=mesh['bond'=32,'outer'=4] {'outer'}, dimensions={0} | all-to-all | bytes 262144 | tf_op jit(solution)/shard_map/all_to_all | solution.py:9
  18.6 0.0 all-gather.2.cloned.1.call-update
  18.6 1.1 reshape.16
  19.7 1.8 pad_maximum_fusion
  21.6 7.8 %all-to-all-start = ((bf16[128,4,384]{2,1,0:T(4,128)(2,1)}), bf16[128,4,384]{2,1,0:T(4,128)(2,1)S(1)}, u32[]{:S(2)}, u32[]{:S(2)}) async-start(bf16[128,4,384]{2,1,0:T(4,128)(2,1)} %pad_maximum_fusion), calls=%async_computation | async-start | bytes 786432 | tf_op jit(solution)/shard_map/all_to_all | solution.py:29
  29.4 10.5 %all-to-all-done = bf16[128,4,384]{2,1,0:T(4,128)(2,1)S(1)} async-done(((bf16[128,4,384]{2,1,0:T(4,128)(2,1)}), bf16[128,4,384]{2,1,0:T(4,128)(2,1)S(1)}, u32[]{:S(2)}, u32[]{:S(2)}) %all-to-all-start) | async-done | bytes 393248 | tf_op jit(solution)/shard_map/all_to_all | solution.py:29
  39.9 0.2 copy.21
  40.0 0.1 slice.8
  40.2 0.2 copy.30
  40.4 0.1 copy.23
  40.6 135.7 %all-gather.2.cloned.1.call-done = bf16[16384,128]{1,0:T(8,128)(2,1)} async-done(((bf16[512,128]{1,0:T(8,128)(2,1)}), bf16[16384,128]{1,0:T(8,128)(2,1)}) %all-gather.2.cloned.1.call-update) | async-done | bytes 4194320 | tf_op jit(solution)/shard_map/all_gather | solution.py:53
  176.3 67.8 %while.14 = (s32[]{:T(128)}, f32[128,2,128]{2,0,1:T(8,128)S(1)}, bf16[4,128,2,128]{1,3,2,0:T(8,128)(2,1)S(1)}, bf16[4,128,128]{1,2,0:T(8,128)(2,1)S(1)}, bf16[12...) while((s32[]{:T(128)}, f32[128,2,128]{2,0,1:T(8,128)S(1)}, ...), condition=%wide.region_1.2_spmd.clone, body=%wide.region_0.1_spmd.clone.sunk | while | flops 2690711552 | bytes 17137760 | solution.py:75
  176.3 7.5 %fusion.52 = bf16[128,128,128]{2,0,1:T(8,128)(2,1)} fusion(bf16[128,128,128]{2,1,0:T(8,128)(2,1)} %get-tuple-element.192, bf16[4,128,128]{1,2,0:T(8,128)(2,1)S(1)} %get-tuple-element.191, s32[]{:T(128)} %get-tuple-element.181), kind=kOutput, calls=%fused_computation.9.clone.1 | convolution fusion | flops 538968064 | bytes 8421380 | tf_op jit(solution)/shard_map/while/body/eval_jaxpr/lr,lkx->rkx/dot_general | solution.py:64
  183.8 9.4 %fusion.53 = f32[128,2,128]{2,0,1:T(8,128)S(1)} fusion(bf16[128,128,128]{2,1,0:T(8,128)(2,1)} %get-tuple-element.192, bf16[128,128,128]{2,0,1:T(8,128)(2,1)} %fusion.52, f32[128,2,128]{2,0,1:T(8,128)S(1)} %get-tuple-element.182, bf16[4,128,2,128]{1,3,2,0:T(8,128)(2,1)S(1)} %get-tuple-element.190, s32[]{:T(128)} %get-tuple-element.181, pred[]{:T(512)S(6)} %compare.3), kind=kOutput, calls=%fused_computation.11.clone.1 | convolution fusion | flops 2151743488 | bytes 8716293 | tf_op jit(solution)/shard_map/while/body/eval_jaxpr/drxs,rsy->xdy/dot_general | solution.py:70
  193.3 7.5 %fusion.52 = bf16[128,128,128]{2,0,1:T(8,128)(2,1)} fusion(bf16[128,128,128]{2,1,0:T(8,128)(2,1)} %get-tuple-element.192, bf16[4,128,128]{1,2,0:T(8,128)(2,1)S(1)} %get-tuple-element.191, s32[]{:T(128)} %get-tuple-element.181), kind=kOutput, calls=%fused_computation.9.clone.1 | convolution fusion | flops 538968064 | bytes 8421380 | tf_op jit(solution)/shard_map/while/body/eval_jaxpr/lr,lkx->rkx/dot_general | solution.py:64
  200.8 9.4 %fusion.53 = f32[128,2,128]{2,0,1:T(8,128)S(1)} fusion(bf16[128,128,128]{2,1,0:T(8,128)(2,1)} %get-tuple-element.192, bf16[128,128,128]{2,0,1:T(8,128)(2,1)} %fusion.52, f32[128,2,128]{2,0,1:T(8,128)S(1)} %get-tuple-element.182, bf16[4,128,2,128]{1,3,2,0:T(8,128)(2,1)S(1)} %get-tuple-element.190, s32[]{:T(128)} %get-tuple-element.181, pred[]{:T(512)S(6)} %compare.3), kind=kOutput, calls=%fused_computation.11.clone.1 | convolution fusion | flops 2151743488 | bytes 8716293 | tf_op jit(solution)/shard_map/while/body/eval_jaxpr/drxs,rsy->xdy/dot_general | solution.py:70
  210.2 7.5 %fusion.52 = bf16[128,128,128]{2,0,1:T(8,128)(2,1)} fusion(bf16[128,128,128]{2,1,0:T(8,128)(2,1)} %get-tuple-element.192, bf16[4,128,128]{1,2,0:T(8,128)(2,1)S(1)} %get-tuple-element.191, s32[]{:T(128)} %get-tuple-element.181), kind=kOutput, calls=%fused_computation.9.clone.1 | convolution fusion | flops 538968064 | bytes 8421380 | tf_op jit(solution)/shard_map/while/body/eval_jaxpr/lr,lkx->rkx/dot_general | solution.py:64
  217.7 9.4 %fusion.53 = f32[128,2,128]{2,0,1:T(8,128)S(1)} fusion(bf16[128,128,128]{2,1,0:T(8,128)(2,1)} %get-tuple-element.192, bf16[128,128,128]{2,0,1:T(8,128)(2,1)} %fusion.52, f32[128,2,128]{2,0,1:T(8,128)S(1)} %get-tuple-element.182, bf16[4,128,2,128]{1,3,2,0:T(8,128)(2,1)S(1)} %get-tuple-element.190, s32[]{:T(128)} %get-tuple-element.181, pred[]{:T(512)S(6)} %compare.3), kind=kOutput, calls=%fused_computation.11.clone.1 | convolution fusion | flops 2151743488 | bytes 8716293 | tf_op jit(solution)/shard_map/while/body/eval_jaxpr/drxs,rsy->xdy/dot_general | solution.py:70
  227.1 7.5 %fusion.52 = bf16[128,128,128]{2,0,1:T(8,128)(2,1)} fusion(bf16[128,128,128]{2,1,0:T(8,128)(2,1)} %get-tuple-element.192, bf16[4,128,128]{1,2,0:T(8,128)(2,1)S(1)} %get-tuple-element.191, s32[]{:T(128)} %get-tuple-element.181), kind=kOutput, calls=%fused_computation.9.clone.1 | convolution fusion | flops 538968064 | bytes 8421380 | tf_op jit(solution)/shard_map/while/body/eval_jaxpr/lr,lkx->rkx/dot_general | solution.py:64
  234.7 9.4 %fusion.53 = f32[128,2,128]{2,0,1:T(8,128)S(1)} fusion(bf16[128,128,128]{2,1,0:T(8,128)(2,1)} %get-tuple-element.192, bf16[128,128,128]{2,0,1:T(8,128)(2,1)} %fusion.52, f32[128,2,128]{2,0,1:T(8,128)S(1)} %get-tuple-element.182, bf16[4,128,2,128]{1,3,2,0:T(8,128)(2,1)S(1)} %get-tuple-element.190, s32[]{:T(128)} %get-tuple-element.181, pred[]{:T(512)S(6)} %compare.3), kind=kOutput, calls=%fused_computation.11.clone.1 | convolution fusion | flops 2151743488 | bytes 8716293 | tf_op jit(solution)/shard_map/while/body/eval_jaxpr/drxs,rsy->xdy/dot_general | solution.py:70
  244.1 14.5 %all_to_all.29 = f32[32,4,2,128]{3,1,2,0:T(4,128)S(1)} all-to-all(f32[32,4,2,128]{3,1,2,0:T(4,128)S(1)} %copy.24), channel_id=1, replica_groups=mesh['bond'=32,'outer'=4] {'bond'}, dimensions={0} | all-to-all | bytes 262144 | tf_op jit(solution)/shard_map/all_to_all | solution.py:47
  258.7 0.6 copy.26
  (4 shorter events, 0.1 us)
Async XLA Ops:
  6.5 169.8 %all-gather.2.cloned.1.call-start = ((), (), s32[]{:S(2)}) async-start(), calls=%async_computation.3 | async-start | bytes 4325376 | tf_op jit(solution)/shard_map/all_gather | solution.py:53
  21.6 18.3 %all-to-all-start = ((bf16[128,4,384]{2,1,0:T(4,128)(2,1)}), bf16[128,4,384]{2,1,0:T(4,128)(2,1)S(1)}, u32[]{:S(2)}, u32[]{:S(2)}) async-start(bf16[128,4,384]{2,1,0:T(4,128)(2,1)} %pad_maximum_fusion), calls=%async_computation | async-start | bytes 786432 | tf_op jit(solution)/shard_map/all_to_all | solution.py:29
Sparse Core Ops, SparseCore 0:
  18.7 157.5 all-gather.1
where the time goes:
time: 267 us; the launch traced here: 266 us
  waiting for transfers between devices  146 us (55%)
  matrix products  67.7 us (25%)
  blocking collectives  25.8 us (10%)
  between operations  13.5 us (5%)
  starting transfers between devices  7.78 us (3%)
  local copies, waits for them, and re-layouts  3.18 us (1%)
    all_gather x1, waiting for transfers between devices, on_device(): gathered = lax.all_gather(grouped, 'bond', axis=0, tiled=True)  136 us
    dot_general x4, matrix products, member(): jnp.einsum('drxs,rsy->xdy', paired, iso_full, preferred_element_type=jnp....  37.5 us
    dot_general x4, matrix products, member(): jnp.einsum('lr,lkx->rkx', upper_slab, iso_full, preferred_element_type=jn...  30.1 us
    all_to_all x1, blocking collectives, sum_at_owner(): tiles = lax.all_to_all(split_up(value, dim, peers), axis, 0, 0, tiled=True)  14.5 us
    all_to_all x1, blocking collectives, from_everyone(): lax.all_to_all(jnp.broadcast_to(value[None], (peers, *value.shape)), axis...  11.3 us
    all_to_all x1, waiting for transfers between devices, side_by_side(): lax.all_to_all(both, axis, split_axis=split_dim, concat_axis=concat_dim,...  10.5 us
    all_to_all x1, starting transfers between devices, side_by_side(): lax.all_to_all(both, axis, split_axis=split_dim, concat_axis=concat_dim,...  7.77 us
  transfers between devices with their start and end apart: 2, of which 2 were waited for; matrix products, arithmetic and copies ran while one was open for 1% of the time, Pallas kernels for 0%

commit v1 on v0

--- a/solution.py
+++ b/solution.py
@@ -50,7 +50,9 @@
 
 def on_device(upper, lower, isometry):
     grouped = gathered_copies(isometry, "outer", 0)
-    gathered = lax.all_gather(grouped, "bond", axis=0, tiled=True)
+    part_now = jnp.stack(jax.lax.axis_size("bond") * [grouped], 0)
+    long_array = jax.lax.all_to_all(part_now, "bond", 0, 0)
+    gathered = jnp.concatenate(long_array, 0)
     upper_local, lower_local = side_by_side((upper, lower), "bond", 0, 1, 2)
     width = gathered.shape[1]
     iso_full = gathered.reshape(width, width, width)

time: 267 us -> 179 us (0.67)
  waiting for transfers between devices: 146 us -> 60.7 us
  between operations: 13.5 us -> 0.08 us
  blocking collectives: 25.8 us -> 31.9 us
  local copies, waits for them, and re-layouts: 3.18 us -> 6.74 us
    all_gather x1 -> x0, waiting for transfers between devices: 136 us -> none  [on_device(): gathered = lax.all_gather(grouped, 'bond', axis=0, tiled=True)]
    all_to_all x1 -> x2, waiting for transfers between devices: 10.5 us -> 60.7 us  [the longest x1 56.8 us: on_device(): long_array = jax.lax.all_to_all(part_now, 'bond', 0, 0)]
    all_to_all x1, blocking collectives: 11.3 us -> 17.7 us  [side_by_side(): lax.all_to_all(both, axis, split_axis=split_dim, concat_axis=concat_dim,...]
    another operation x0 -> x1, local copies, waits for them, and re-layouts: none -> 2.92 us  [on_device(): part_now = jnp.stack(jax.lax.axis_size('bond') * [grouped], 0)]
    all_to_all x1 -> x2, starting transfers between devices: 7.77 us -> 10.1 us  [the longest x1 5.26 us: from_everyone(): lax.all_to_all(jnp.broadcast_to(value[None], (peers, *value.shape)), axis...]
  transfers between devices with their start and end apart: 2 -> 2, of which waited for: 2 -> 2; matrix products, arithmetic and copies ran while one was open for 1% -> 2% of each run, Pallas kernels for 0% -> 0%
where the time goes in v1:
time: 179 us; the launch traced here: 178 us
  matrix products  67.7 us (38%)
  waiting for transfers between devices  60.7 us (34%)
  blocking collectives  31.9 us (18%)
  starting transfers between devices  10.1 us (6%)
  local copies, waits for them, and re-layouts  6.74 us (4%)
    all_to_all x1, waiting for transfers between devices, on_device(): long_array = jax.lax.all_to_all(part_now, 'bond', 0, 0)  56.8 us
    dot_general x4, matrix products, member(): jnp.einsum('drxs,rsy->xdy', paired, iso_full, preferred_element_type=jnp....  37.5 us
    dot_general x4, matrix products, member(): jnp.einsum('lr,lkx->rkx', upper_slab, iso_full, preferred_element_type=jn...  30.2 us
    all_to_all x1, blocking collectives, side_by_side(): lax.all_to_all(both, axis, split_axis=split_dim, concat_axis=concat_dim,...  17.7 us
    all_to_all x1, blocking collectives, sum_at_owner(): tiles = lax.all_to_all(split_up(value, dim, peers), axis, 0, 0, tiled=True)  14.2 us
    all_to_all x1, starting transfers between devices, from_everyone(): lax.all_to_all(jnp.broadcast_to(value[None], (peers, *value.shape)), axis...  5.26 us
    all_to_all x1, starting transfers between devices, on_device(): long_array = jax.lax.all_to_all(part_now, 'bond', 0, 0)  4.86 us
    all_to_all x1, waiting for transfers between devices, from_everyone(): lax.all_to_all(jnp.broadcast_to(value[None], (peers, *value.shape)), axis...  3.9 us
  transfers between devices with their start and end apart: 2, of which 2 were waited for; matrix products, arithmetic and copies ran while one was open for 2% of the time, Pallas kernels for 0%

profile of v1, /device:TPU:0, one launch (start us, length us, event | category | flops | bytes accessed | tf_op | source)
XLA Modules:
  0.0 178.4 jit_solution(13680053936250075184)
XLA Ops:
  0.0 1.4 broadcast_in_dim.10
  1.4 5.3 %all-to-all-start.1 = ((bf16[4,128,128]{2,1,0:T(8,128)(2,1)}), bf16[4,128,128]{2,1,0:T(8,128)(2,1)S(1)}, u32[]{:S(2)}, u32[]{:S(2)}) async-start(bf16[4,128,128]{2,1,0:T(8,128)(2,1)} %broadcast_in_dim.10), calls=%async_computation.1 | async-start | bytes 262144 | tf_op jit(solution)/shard_map/all_to_all | solution.py:9
  6.7 1.1 reshape.12
  7.8 1.1 pad_maximum_fusion
  8.9 3.9 %all-to-all-done.1 = bf16[4,128,128]{2,1,0:T(8,128)(2,1)S(1)} async-done(((bf16[4,128,128]{2,1,0:T(8,128)(2,1)}), bf16[4,128,128]{2,1,0:T(8,128)(2,1)S(1)}, u32[]{:S(2)}, u32[]{:S(2)}) %all-to-all-start.1) | async-done | bytes 131104 | tf_op jit(solution)/shard_map/all_to_all | solution.py:9
  12.8 17.7 %all_to_all.33 = bf16[128,4,384]{2,1,0:T(4,128)(2,1)S(1)} all-to-all(bf16[128,4,384]{2,1,0:T(4,128)(2,1)S(1)} %pad_maximum_fusion), channel_id=1, replica_groups=mesh['bond'=32,'outer'=4] {'bond'}, dimensions={0} | all-to-all | bytes 786432 | tf_op jit(solution)/shard_map/all_to_all | solution.py:29
  30.5 2.9 %stack.3 = bf16[32,512,128]{2,1,0:T(8,128)(2,1)} broadcast(bf16[512,128]{1,0:T(8,128)(2,1)S(1)} %bitcast.63), dimensions={1,2} | broadcast | bytes 4325376 | tf_op jit(solution)/shard_map/stack | solution.py:53
  33.4 4.9 %all-to-all-start.2 = ((bf16[32,512,128]{2,1,0:T(8,128)(2,1)}), bf16[32,512,128]{2,1,0:T(8,128)(2,1)}, u32[]{:S(2)}, u32[]{:S(2)}) async-start(bf16[32,512,128]{2,1,0:T(8,128)(2,1)} %stack.3), calls=%async_computation.2 | async-start | bytes 8388608 | tf_op jit(solution)/shard_map/all_to_all | solution.py:54
  38.3 0.2 copy.21
  38.5 0.1 slice.8
  38.6 0.2 copy.30
  38.8 0.1 copy.23
  39.0 56.8 %all-to-all-done.2 = bf16[32,512,128]{2,1,0:T(8,128)(2,1)} async-done(((bf16[32,512,128]{2,1,0:T(8,128)(2,1)}), bf16[32,512,128]{2,1,0:T(8,128)(2,1)}, u32[]{:S(2)}, u32[]{:S(2)}) %all-to-all-start.2) | async-done | bytes 4194336 | tf_op jit(solution)/shard_map/all_to_all | solution.py:54
  95.8 67.8 %while.14 = (s32[]{:T(128)}, f32[128,2,128]{2,0,1:T(8,128)S(1)}, bf16[4,128,2,128]{1,3,2,0:T(8,128)(2,1)S(1)}, bf16[4,128,128]{1,2,0:T(8,128)(2,1)S(1)}, bf16[12...) while((s32[]{:T(128)}, f32[128,2,128]{2,0,1:T(8,128)S(1)}, ...), condition=%wide.region_1.2_spmd.clone, body=%wide.region_0.1_spmd.clone.sunk | while | flops 2690711552 | bytes 17137760 | solution.py:77
  95.8 7.5 %fusion.52 = bf16[128,128,128]{2,0,1:T(8,128)(2,1)} fusion(bf16[128,128,128]{2,1,0:T(8,128)(2,1)} %get-tuple-element.192, bf16[4,128,128]{1,2,0:T(8,128)(2,1)S(1)} %get-tuple-element.191, s32[]{:T(128)} %get-tuple-element.181), kind=kOutput, calls=%fused_computation.9.clone.1 | convolution fusion | flops 538968064 | bytes 8421380 | tf_op jit(solution)/shard_map/while/body/eval_jaxpr/lr,lkx->rkx/dot_general | solution.py:66
  103.3 9.4 %fusion.53 = f32[128,2,128]{2,0,1:T(8,128)S(1)} fusion(bf16[128,128,128]{2,1,0:T(8,128)(2,1)} %get-tuple-element.192, bf16[128,128,128]{2,0,1:T(8,128)(2,1)} %fusion.52, f32[128,2,128]{2,0,1:T(8,128)S(1)} %get-tuple-element.182, bf16[4,128,2,128]{1,3,2,0:T(8,128)(2,1)S(1)} %get-tuple-element.190, s32[]{:T(128)} %get-tuple-element.181, pred[]{:T(512)S(6)} %compare.3), kind=kOutput, calls=%fused_computation.11.clone.1 | convolution fusion | flops 2151743488 | bytes 8716293 | tf_op jit(solution)/shard_map/while/body/eval_jaxpr/drxs,rsy->xdy/dot_general | solution.py:72
  112.7 7.5 %fusion.52 = bf16[128,128,128]{2,0,1:T(8,128)(2,1)} fusion(bf16[128,128,128]{2,1,0:T(8,128)(2,1)} %get-tuple-element.192, bf16[4,128,128]{1,2,0:T(8,128)(2,1)S(1)} %get-tuple-element.191, s32[]{:T(128)} %get-tuple-element.181), kind=kOutput, calls=%fused_computation.9.clone.1 | convolution fusion | flops 538968064 | bytes 8421380 | tf_op jit(solution)/shard_map/while/body/eval_jaxpr/lr,lkx->rkx/dot_general | solution.py:66
  120.3 9.4 %fusion.53 = f32[128,2,128]{2,0,1:T(8,128)S(1)} fusion(bf16[128,128,128]{2,1,0:T(8,128)(2,1)} %get-tuple-element.192, bf16[128,128,128]{2,0,1:T(8,128)(2,1)} %fusion.52, f32[128,2,128]{2,0,1:T(8,128)S(1)} %get-tuple-element.182, bf16[4,128,2,128]{1,3,2,0:T(8,128)(2,1)S(1)} %get-tuple-element.190, s32[]{:T(128)} %get-tuple-element.181, pred[]{:T(512)S(6)} %compare.3), kind=kOutput, calls=%fused_computation.11.clone.1 | convolution fusion | flops 2151743488 | bytes 8716293 | tf_op jit(solution)/shard_map/while/body/eval_jaxpr/drxs,rsy->xdy/dot_general | solution.py:72
  129.7 7.5 %fusion.52 = bf16[128,128,128]{2,0,1:T(8,128)(2,1)} fusion(bf16[128,128,128]{2,1,0:T(8,128)(2,1)} %get-tuple-element.192, bf16[4,128,128]{1,2,0:T(8,128)(2,1)S(1)} %get-tuple-element.191, s32[]{:T(128)} %get-tuple-element.181), kind=kOutput, calls=%fused_computation.9.clone.1 | convolution fusion | flops 538968064 | bytes 8421380 | tf_op jit(solution)/shard_map/while/body/eval_jaxpr/lr,lkx->rkx/dot_general | solution.py:66
  137.2 9.4 %fusion.53 = f32[128,2,128]{2,0,1:T(8,128)S(1)} fusion(bf16[128,128,128]{2,1,0:T(8,128)(2,1)} %get-tuple-element.192, bf16[128,128,128]{2,0,1:T(8,128)(2,1)} %fusion.52, f32[128,2,128]{2,0,1:T(8,128)S(1)} %get-tuple-element.182, bf16[4,128,2,128]{1,3,2,0:T(8,128)(2,1)S(1)} %get-tuple-element.190, s32[]{:T(128)} %get-tuple-element.181, pred[]{:T(512)S(6)} %compare.3), kind=kOutput, calls=%fused_computation.11.clone.1 | convolution fusion | flops 2151743488 | bytes 8716293 | tf_op jit(solution)/shard_map/while/body/eval_jaxpr/drxs,rsy->xdy/dot_general | solution.py:72
  146.6 7.5 %fusion.52 = bf16[128,128,128]{2,0,1:T(8,128)(2,1)} fusion(bf16[128,128,128]{2,1,0:T(8,128)(2,1)} %get-tuple-element.192, bf16[4,128,128]{1,2,0:T(8,128)(2,1)S(1)} %get-tuple-element.191, s32[]{:T(128)} %get-tuple-element.181), kind=kOutput, calls=%fused_computation.9.clone.1 | convolution fusion | flops 538968064 | bytes 8421380 | tf_op jit(solution)/shard_map/while/body/eval_jaxpr/lr,lkx->rkx/dot_general | solution.py:66
  154.2 9.4 %fusion.53 = f32[128,2,128]{2,0,1:T(8,128)S(1)} fusion(bf16[128,128,128]{2,1,0:T(8,128)(2,1)} %get-tuple-element.192, bf16[128,128,128]{2,0,1:T(8,128)(2,1)} %fusion.52, f32[128,2,128]{2,0,1:T(8,128)S(1)} %get-tuple-element.182, bf16[4,128,2,128]{1,3,2,0:T(8,128)(2,1)S(1)} %get-tuple-element.190, s32[]{:T(128)} %get-tuple-element.181, pred[]{:T(512)S(6)} %compare.3), kind=kOutput, calls=%fused_computation.11.clone.1 | convolution fusion | flops 2151743488 | bytes 8716293 | tf_op jit(solution)/shard_map/while/body/eval_jaxpr/drxs,rsy->xdy/dot_general | solution.py:72
  163.6 14.2 %all_to_all.34 = f32[32,4,2,128]{3,1,2,0:T(4,128)S(1)} all-to-all(f32[32,4,2,128]{3,1,2,0:T(4,128)S(1)} %copy.24), channel_id=1, replica_groups=mesh['bond'=32,'outer'=4] {'bond'}, dimensions={0} | all-to-all | bytes 262144 | tf_op jit(solution)/shard_map/all_to_all | solution.py:47
  177.8 0.6 copy.26
  (4 shorter events, 0.1 us)
Async XLA Ops:
  1.4 11.4 %all-to-all-start.1 = ((bf16[4,128,128]{2,1,0:T(8,128)(2,1)}), bf16[4,128,128]{2,1,0:T(8,128)(2,1)S(1)}, u32[]{:S(2)}, u32[]{:S(2)}) async-start(bf16[4,128,128]{2,1,0:T(8,128)(2,1)} %broadcast_in_dim.10), calls=%async_computation.1 | async-start | bytes 262144 | tf_op jit(solution)/shard_map/all_to_all | solution.py:9
  33.4 62.4 %all-to-all-start.2 = ((bf16[32,512,128]{2,1,0:T(8,128)(2,1)}), bf16[32,512,128]{2,1,0:T(8,128)(2,1)}, u32[]{:S(2)}, u32[]{:S(2)}) async-start(bf16[32,512,128]{2,1,0:T(8,128)(2,1)} %stack.3), calls=%async_computation.2 | async-start | bytes 8388608 | tf_op jit(solution)/shard_map/all_to_all | solution.py:54
